TPU v7x, 32 devices: a whole 2x2x4 slice. The times are simulated.
32 devices in a mesh: gz: 16 (over z, y, x), gy: 2 (over core).
Axes of the slice: x: 2, y: 2, z: 4, core: 2. Of those that a mesh axis runs over, the one named last changes fastest.
Arguments:
- snapshots: float32 [48, 64, 128, 256], P(None, 'gz', 'gy'), may hold values from -6 to 6
- energies: float32 [48], replicated, may hold values from 0.3 to 3
- plane_weight: float32 [64], P('gz'), may hold values from 1 to 10
Outputs:
- modes: float32 [16, 64, 128, 256], P(None, 'gz', 'gy')
- basis: float32 [48, 16], replicated
All inputs are finite; a program needn't handle non-finite values.
Results may differ from a plain program's by a relative error of at most 0.0003.
Values sent between devices are 32-bit elements; how exact they have to be, the bound alone decides.
A program may use at most 128 MiB of HBM per device.

v0:
```python
import jax
import jax.numpy as jnp
from jax import lax
from jax.sharding import PartitionSpec as P

MODES = 16
ITERS = 6


def padded_2(block, sides, width):
    for axis, dim in sides:
        count = lax.axis_size(axis)
        forward = [(i, i + 1) for i in range(count - 1)]
        forward.append((count - 1, 0))
        backward = [(target, source) for source, target in forward]
        low = lax.ppermute(
            lax.slice_in_dim(block, block.shape[dim] - width, None, axis=dim), axis, forward
        )
        high = lax.ppermute(lax.slice_in_dim(block, 0, width, axis=dim), axis, backward)
        block = jnp.concatenate([low, block, high], axis=dim)
    return block


def local(snapshots, energies, plane_weight):
    count, planes, rows, width = snapshots.shape
    total = planes * lax.axis_size("gz") * rows * lax.axis_size("gy") * width
    scaled = snapshots * energies[:, None, None, None]
    padded = padded_2(scaled, (("gz", 1),), 1)
    filtered = 0.25 * padded[:, :-2] + 0.5 * scaled + 0.25 * padded[:, 2:]
    flat = filtered.reshape(count, -1)
    weighted = (filtered * plane_weight[None, :, None, None]).reshape(count, -1)
    partial_value = jnp.dot(weighted, flat.T, precision=lax.Precision.HIGHEST) / total
    gram = lax.psum(partial_value, ("gz", "gy"))
    basis = jnp.eye(count, dtype=jnp.float32)[:, :MODES]
    for step in range(ITERS):
        image = jnp.dot(gram, basis, precision=lax.Precision.HIGHEST)
        factor = jnp.linalg.cholesky(jnp.dot(image.T, image, precision=lax.Precision.HIGHEST))
        basis = jax.scipy.linalg.solve_triangular(factor, image.T, lower=True).T
    raw = jnp.dot(basis.T, flat, precision=lax.Precision.HIGHEST).reshape(
        MODES, planes, rows, width
    )
    projected = jnp.dot(gram, basis, precision=lax.Precision.HIGHEST)
    norms = jnp.sum(basis * projected, axis=0)
    modes = raw / jnp.sqrt(norms)[:, None, None, None]
    return (modes, basis)


def solution(mesh):
    placed = (P(None, "gz", "gy", None), P(), P("gz"))
    return jax.shard_map(
        local,
        mesh=mesh,
        in_specs=placed,
        out_specs=(P(None, "gz", "gy", None), P()),
        check_vma=False,
    )
```

profile of v0, /device:TPU:0, one launch (start us, length us, event | category | flops | bytes accessed | tf_op | source)
XLA Modules:
  0.0 292.3 jit_solution(18266743144551200550)
XLA Ops:
  0.6 12.0 %broadcast_multiply_fusion.1 = f32[48,4,64,256]{3,2,1,0:T(8,128)} fusion(f32[48,4,64,256]{3,2,1,0:T(8,128)} %param.6, f32[48]{0:T(128)} %param.7), kind=kLoop, calls=%fused_computation.12 | loop fusion | flops 3145728 | bytes 25166016 | tf_op jit(solution)/shard_map/mul | solution.py:27
  12.7 3.7 %fusion.67 = (f32[48,1,64,256]{3,2,1,0:T(8,128)S(1)}, f32[48,1,64,256]{3,2,1,0:T(8,128)S(1)}) fusion(f32[48,4,64,256]{3,2,1,0:T(8,128)} %broadcast_multiply_fusion.1), kind=kLoop, calls=%fused_computation.84 | loop fusion | bytes 12582912 | tf_op jit(solution)/shard_map/slice | solution.py:17
  16.4 3.0 %collective-permute-start = (f32[48,1,64,256]{3,2,1,0:T(8,128)S(1)}, f32[48,1,64,256]{3,2,1,0:T(8,128)}, u32[]{:S(2)}, u32[]{:S(2)}) collective-permute-start(f32[48,1,64,256]{3,2,1,0:T(8,128)S(1)} %get-tuple-element.10), channel_id=1, source_target_pairs={{0,2},{2,4},{4,6},{6,8},{8,10},{10,12},{12,14},{14,16},{16,18},{18... | collective-permute-start | bytes 9437192 | tf_op jit(solution)/shard_map/ppermute | solution.py:16
  19.4 4.1 %collective-permute-start.1 = (f32[48,1,64,256]{3,2,1,0:T(8,128)S(1)}, f32[48,1,64,256]{3,2,1,0:T(8,128)}, u32[]{:S(2)}, u32[]{:S(2)}) collective-permute-start(f32[48,1,64,256]{3,2,1,0:T(8,128)S(1)} %get-tuple-element.11), channel_id=1, source_target_pairs={{2,0},{4,2},{6,4},{8,6},{10,8},{12,10},{14,12},{16,14},{18,16},{20... | collective-permute-start | bytes 9437192 | tf_op jit(solution)/shard_map/ppermute | solution.py:19
  23.5 130.7 %collective-permute-done = f32[48,1,64,256]{3,2,1,0:T(8,128)} collective-permute-done((f32[48,1,64,256]{3,2,1,0:T(8,128)S(1)}, f32[48,1,64,256]{3,2,1,0:T(8,128)}, u32[]{:S(2)}, u32[]{:S(2)}) %collective-permute-start) | collective-permute-done | bytes 3145760 | tf_op jit(solution)/shard_map/ppermute | solution.py:16
  154.2 2.1 collective-permute-done.1
  156.3 13.5 %broadcast_multiply_fusion = (f32[48,4,64,256]{3,2,1,0:T(8,128)}, f32[48,4,64,256]{3,2,1,0:T(8,128)}) fusion(f32[4]{0:T(128)S(1)} %copy-done.2, f32[48,1,64,256]{3,2,1,0:T(8,128)} %collective-permute-done.1, f32[48,4,64,256]{3,2,1,0:T(8,128)S(1)} %copy-done, f32[48,1,64,256]{3,2,1,0:T(8,128)} %collective-permute-done), kind=kLoop, calls=%fused_computation.11 | loop fusion | flops 25165824 | bytes 44040208 | tf_op jit(solution)/shard_map/mul | solution.py:31
  169.7 32.1 %fusion.16 = f32[48,48]{1,0:T(8,128)S(1)} fusion(f32[48,4,64,256]{3,2,1,0:T(8,128)} %get-tuple-element.9, f32[48,4,64,256]{3,2,1,0:T(8,128)} %get-tuple-element.8), kind=kOutput, calls=%fused_computation.15 | convolution fusion | flops 1811941632 | bytes 25175040 | tf_op jit(solution)/shard_map/dot_general | solution.py:32
  201.8 39.7 %psum.7 = f32[48,48]{1,0:T(8,128)S(1)} all-reduce(f32[48,48]{1,0:T(8,128)S(1)} %fusion.16), channel_id=1, replica_groups=mesh['gz'=16,'gy'=2] {'gz','gy'}, use_global_device_ids=true, to_apply=%region_0.0 | all-reduce | flops 2304 | bytes 18432 | tf_op jit(solution)/shard_map/psum | solution.py:33
  241.6 0.2 fusion.22
  242.0 1.5 cholesky.104
  243.5 0.6 compare_reduce_fusion.5
  244.1 0.6 fusion.24
  244.8 1.2 custom-call.10
  246.0 0.2 fusion.51
  246.2 0.2 fusion.69
  246.6 1.5 cholesky.115
  248.1 0.6 compare_reduce_fusion.4
  248.8 0.6 fusion.25
  249.4 1.2 custom-call.11
  250.6 0.2 fusion.47
  250.8 0.2 fusion.71
  251.2 1.5 cholesky.126
  252.7 0.6 compare_reduce_fusion.3
  253.4 0.6 fusion.26
  254.0 1.2 custom-call.12
  255.3 0.2 fusion.43
  255.5 0.2 fusion.73
  255.8 1.5 cholesky.137
  257.4 0.6 compare_reduce_fusion.2
  258.0 0.6 fusion.27
  258.7 1.2 custom-call.13
  259.9 0.2 fusion.39
  260.1 0.2 fusion.75
  260.5 1.5 cholesky.148
  262.0 0.6 compare_reduce_fusion.1
  262.6 0.6 fusion.28
  263.3 1.2 custom-call.14
  264.5 0.2 fusion.35
  264.7 0.2 fusion.77
  265.1 1.5 cholesky.159
  266.6 0.6 compare_reduce_fusion
  267.2 0.6 fusion.29
  267.9 1.2 custom-call.15
  269.1 0.2 fusion.31
  269.3 0.3 fusion.21
  269.6 18.2 %broadcast_divide_fusion = f32[16,4,64,256]{3,0,2,1:T(8,128)S(1)} fusion(f32[16]{0:T(128)S(1)} %sqrt.7, f32[4,64,256,48]{2,1,0,3:T(8,128)} %bitcast.120, f32[16,48]{1,0:T(8,128)S(1)} %fusion.31), kind=kOutput, calls=%fused_computation.13 | convolution fusion | flops 605028352 | bytes 16780352 | tf_op jit(solution)/shard_map/dot_general | solution.py:39
  287.8 4.4 %copy.23 = f32[16,4,64,256]{3,2,1,0:T(8,128)} copy(f32[16,4,64,256]{3,0,2,1:T(8,128)S(1)} %broadcast_divide_fusion) | data formatting | bytes 8388608
  (31 shorter events, 1.6 us)
Async XLA Ops:
  12.7 143.6 %copy-start = (f32[48,4,64,256]{3,2,1,0:T(8,128)S(1)}, f32[48,4,64,256]{3,2,1,0:T(8,128)}, u32[]{:S(2)}) copy-start(f32[48,4,64,256]{3,2,1,0:T(8,128)} %broadcast_multiply_fusion.1) | copy-start | bytes 37748740
  12.7 143.6 %copy-start.2 = (f32[4]{0:T(128)S(1)}, f32[4]{0:T(128)}, u32[]{:S(2)}) copy-start(f32[4]{0:T(128)} %param.8) | copy-start | bytes 52
  16.4 137.8 %collective-permute-start = (f32[48,1,64,256]{3,2,1,0:T(8,128)S(1)}, f32[48,1,64,256]{3,2,1,0:T(8,128)}, u32[]{:S(2)}, u32[]{:S(2)}) collective-permute-start(f32[48,1,64,256]{3,2,1,0:T(8,128)S(1)} %get-tuple-element.10), channel_id=1, source_target_pairs={{0,2},{2,4},{4,6},{6,8},{8,10},{10,12},{12,14},{14,16},{16,18},{18... | collective-permute-start | bytes 9437192 | tf_op jit(solution)/shard_map/ppermute | solution.py:16
  19.4 136.8 %collective-permute-start.1 = (f32[48,1,64,256]{3,2,1,0:T(8,128)S(1)}, f32[48,1,64,256]{3,2,1,0:T(8,128)}, u32[]{:S(2)}, u32[]{:S(2)}) collective-permute-start(f32[48,1,64,256]{3,2,1,0:T(8,128)S(1)} %get-tuple-element.11), channel_id=1, source_target_pairs={{2,0},{4,2},{6,4},{8,6},{10,8},{12,10},{14,12},{16,14},{18,16},{20... | collective-permute-start | bytes 9437192 | tf_op jit(solution)/shard_map/ppermute | solution.py:19
  269.3 22.9 %copy-start.1 = (f32[16,48]{1,0:T(8,128)}, f32[16,48]{1,0:T(8,128)S(1)}, u32[]{:S(2)}) copy-start(f32[16,48]{1,0:T(8,128)S(1)} %fusion.31) | copy-start | bytes 9220
where the time goes:
time: 293 us; the launch traced here: 292 us
  waiting for transfers between devices  133 us (45%)
  matrix products  53.6 us (18%)
  other arithmetic  49.7 us (17%)
  blocking collectives  39.7 us (14%)
  local copies, waits for them, and re-layouts  8.63 us (3%)
  starting transfers between devices  7.08 us (2%)
    ppermute x1, waiting for transfers between devices, padded_2(): lax.ppermute(lax.slice_in_dim(block, block.shape[dim] - width, None, axis...  131 us
    psum x1, blocking collectives, local(): gram = lax.psum(partial_value, ('gz', 'gy'))  39.7 us
    dot_general x1, matrix products, local(): jnp.dot(weighted, flat.T, precision=lax.Precision.HIGHEST) / total  32.1 us
    dot_general x1, matrix products, local(): jnp.dot(basis.T, flat, precision=lax.Precision.HIGHEST)  18.2 us
    mul x1, other arithmetic, local(): weighted = (filtered * plane_weight[None, :, None, None]).reshape(count, -1)  13.5 us
    another operation x18, other arithmetic, local(): jnp.linalg.cholesky(jnp.dot(image.T, image, precision=lax.Precision.HIGHE...  12.9 us
    mul x1, other arithmetic, local(): scaled = snapshots * energies[:, None, None, None]  12 us
    another operation x12, other arithmetic, local(): basis = jax.scipy.linalg.solve_triangular(factor, image.T, lower=True).T  11.3 us
  transfers between devices with their start and end apart: 2, of which 2 were waited for; matrix products, arithmetic and copies ran while one was open for 0% of the time, Pallas kernels for 0%

commit v1 on v0

--- a/solution.py
+++ b/solution.py
@@ -30,7 +30,7 @@
     flat = filtered.reshape(count, -1)
     weighted = (filtered * plane_weight[None, :, None, None]).reshape(count, -1)
     partial_value = jnp.dot(weighted, flat.T, precision=lax.Precision.HIGHEST) / total
-    gram = lax.psum(partial_value, ("gz", "gy"))
+    gram = lax.psum(lax.psum(partial_value, "gz"), "gy")
     basis = jnp.eye(count, dtype=jnp.float32)[:, :MODES]
     for step in range(ITERS):
         image = jnp.dot(gram, basis, precision=lax.Precision.HIGHEST)

time: 293 us -> 331 us (1.13)
  blocking collectives: 39.7 us -> 78.3 us
    psum x1 -> x2, blocking collectives: 39.7 us -> 78.3 us  [local(): gram = lax.psum(lax.psum(partial_value, 'gz'), 'gy')]
where the time goes in v1:
time: 331 us
  waiting for transfers between devices  133 us (40%)
  blocking collectives  78.3 us (24%)
  matrix products  53.4 us (16%)
  other arithmetic  49.7 us (15%)
  local copies, waits for them, and re-layouts  8.63 us (3%)
  starting transfers between devices  7.08 us (2%)
    ppermute x1, waiting for transfers between devices, padded_2(): lax.ppermute(lax.slice_in_dim(block, block.shape[dim] - width, None, axis...  131 us
    psum x2, blocking collectives, local(): gram = lax.psum(lax.psum(partial_value, 'gz'), 'gy')  78.3 us
    dot_general x1, matrix products, local(): jnp.dot(weighted, flat.T, precision=lax.Precision.HIGHEST) / total  32.1 us
    dot_general x1, matrix products, local(): jnp.dot(basis.T, flat, precision=lax.Precision.HIGHEST)  17.9 us
    mul x1, other arithmetic, local(): weighted = (filtered * plane_weight[None, :, None, None]).reshape(count, -1)  13.5 us
    another operation x18, other arithmetic, local(): jnp.linalg.cholesky(jnp.dot(image.T, image, precision=lax.Precision.HIGHE...  12.9 us
    mul x1, other arithmetic, local(): scaled = snapshots * energies[:, None, None, None]  12 us
    another operation x12, other arithmetic, local(): basis = jax.scipy.linalg.solve_triangular(factor, image.T, lower=True).T  11.3 us
  transfers between devices with their start and end apart: 2, of which 2 were waited for; matrix products, arithmetic and copies ran while one was open for 0% of the time, Pallas kernels for 0%

profile of v1, /device:TPU:0, one launch (start us, length us, event | category | flops | bytes accessed | tf_op | source)
XLA Modules:
  0.0 330.6 jit_solution(15590672196728312854)
XLA Ops:
  0.6 12.0 %broadcast_multiply_fusion.1 = f32[48,4,64,256]{3,2,1,0:T(8,128)} fusion(f32[48,4,64,256]{3,2,1,0:T(8,128)} %param.6, f32[48]{0:T(128)} %param.7), kind=kLoop, calls=%fused_computation.12 | loop fusion | flops 3145728 | bytes 25166016 | tf_op jit(solution)/shard_map/mul | solution.py:27
  12.7 3.7 %fusion.67 = (f32[48,1,64,256]{3,2,1,0:T(8,128)S(1)}, f32[48,1,64,256]{3,2,1,0:T(8,128)S(1)}) fusion(f32[48,4,64,256]{3,2,1,0:T(8,128)} %broadcast_multiply_fusion.1), kind=kLoop, calls=%fused_computation.84 | loop fusion | bytes 12582912 | tf_op jit(solution)/shard_map/slice | solution.py:17
  16.4 3.0 collective-permute-start
  19.4 4.1 %collective-permute-start.1 = (f32[48,1,64,256]{3,2,1,0:T(8,128)S(1)}, f32[48,1,64,256]{3,2,1,0:T(8,128)}, u32[]{:S(2)}, u32[]{:S(2)}) collective-permute-start(f32[48,1,64,256]{3,2,1,0:T(8,128)S(1)} %get-tuple-element.11), channel_id=1, source_target_pairs={{2,0},{4,2},{6,4},{8,6},{10,8},{12,10},{14,12},{16,14},{18,16},{20... | collective-permute-start | bytes 9437192 | tf_op jit(solution)/shard_map/ppermute | solution.py:19
  23.5 130.7 %collective-permute-done = f32[48,1,64,256]{3,2,1,0:T(8,128)} collective-permute-done((f32[48,1,64,256]{3,2,1,0:T(8,128)S(1)}, f32[48,1,64,256]{3,2,1,0:T(8,128)}, u32[]{:S(2)}, u32[]{:S(2)}) %collective-permute-start) | collective-permute-done | bytes 3145760 | tf_op jit(solution)/shard_map/ppermute | solution.py:16
  154.2 2.1 collective-permute-done.1
  156.3 13.5 %broadcast_multiply_fusion = (f32[48,4,64,256]{3,2,1,0:T(8,128)}, f32[48,4,64,256]{3,2,1,0:T(8,128)}) fusion(f32[4]{0:T(128)S(1)} %copy-done.2, f32[48,1,64,256]{3,2,1,0:T(8,128)} %collective-permute-done.1, f32[48,4,64,256]{3,2,1,0:T(8,128)S(1)} %copy-done, f32[48,1,64,256]{3,2,1,0:T(8,128)} %collective-permute-done), kind=kLoop, calls=%fused_computation.11 | loop fusion | flops 25165824 | bytes 44040208 | tf_op jit(solution)/shard_map/mul | solution.py:31
  169.7 32.1 %fusion.16 = f32[48,48]{1,0:T(8,128)S(1)} fusion(f32[48,4,64,256]{3,2,1,0:T(8,128)} %get-tuple-element.9, f32[48,4,64,256]{3,2,1,0:T(8,128)} %get-tuple-element.8), kind=kOutput, calls=%fused_computation.15 | convolution fusion | flops 1811941632 | bytes 25175040 | tf_op jit(solution)/shard_map/dot_general | solution.py:32
  201.8 74.9 %psum.14 = f32[48,48]{1,0:T(8,128)S(1)} all-reduce(f32[48,48]{1,0:T(8,128)S(1)} %fusion.16), channel_id=1, replica_groups=mesh['gz'=16,'gy'=2] {'gz'}, use_global_device_ids=true, to_apply=%region_0.0 | all-reduce | flops 2304 | bytes 18432 | tf_op jit(solution)/shard_map/psum | solution.py:33
  276.8 3.4 %psum.15 = f32[48,48]{1,0:T(8,128)S(1)} all-reduce(f32[48,48]{1,0:T(8,128)S(1)} %psum.14), channel_id=1, replica_groups=mesh['gz'=16,'gy'=2] {'gy'}, use_global_device_ids=true, to_apply=%region_1.0 | all-reduce | flops 2304 | bytes 18432 | tf_op jit(solution)/shard_map/psum | solution.py:33
  280.2 0.2 fusion.22
  280.6 1.5 cholesky.104
  282.1 0.6 compare_reduce_fusion.5
  282.7 0.6 fusion.24
  283.4 1.2 custom-call.10
  284.6 0.2 fusion.51
  284.8 0.2 fusion.69
  285.2 1.5 cholesky.115
  286.7 0.6 compare_reduce_fusion.4
  287.3 0.6 fusion.25
  288.0 1.2 custom-call.11
  289.2 0.2 fusion.47
  289.4 0.2 fusion.71
  289.8 1.5 cholesky.126
  291.3 0.6 compare_reduce_fusion.3
  292.0 0.6 fusion.26
  292.6 1.2 custom-call.12
  293.9 0.2 fusion.43
  294.1 0.2 fusion.73
  294.4 1.5 cholesky.137
  295.9 0.6 compare_reduce_fusion.2
  296.6 0.6 fusion.27
  297.2 1.2 custom-call.13
  298.5 0.2 fusion.39
  298.7 0.2 fusion.75
  299.1 1.5 cholesky.148
  300.6 0.6 compare_reduce_fusion.1
  301.2 0.6 fusion.28
  301.9 1.2 custom-call.14
  303.1 0.2 fusion.35
  303.7 1.5 cholesky.159
  305.2 0.6 compare_reduce_fusion
  305.8 0.6 fusion.29
  306.5 1.2 custom-call.15
  307.7 0.2 fusion.31
  307.9 0.3 fusion.21
  308.2 17.9 %broadcast_divide_fusion = f32[16,4,64,256]{3,0,2,1:T(8,128)S(1)} fusion(f32[16]{0:T(128)S(1)} %sqrt.7, f32[4,64,256,48]{2,1,0,3:T(8,128)} %bitcast.120, f32[16,48]{1,0:T(8,128)S(1)} %fusion.31), kind=kOutput, calls=%fused_computation.13 | convolution fusion | flops 605028352 | bytes 16780352 | tf_op jit(solution)/shard_map/dot_general | solution.py:39
  326.1 4.4 %copy.23 = f32[16,4,64,256]{3,2,1,0:T(8,128)} copy(f32[16,4,64,256]{3,0,2,1:T(8,128)S(1)} %broadcast_divide_fusion) | data formatting | bytes 8388608
  (32 shorter events, 1.7 us)
Async XLA Ops:
  12.7 143.6 %copy-start = (f32[48,4,64,256]{3,2,1,0:T(8,128)S(1)}, f32[48,4,64,256]{3,2,1,0:T(8,128)}, u32[]{:S(2)}) copy-start(f32[48,4,64,256]{3,2,1,0:T(8,128)} %broadcast_multiply_fusion.1) | copy-start | bytes 37748740
  12.7 143.6 %copy-start.2 = (f32[4]{0:T(128)S(1)}, f32[4]{0:T(128)}, u32[]{:S(2)}) copy-start(f32[4]{0:T(128)} %param.8) | copy-start | bytes 52
  16.4 137.8 %collective-permute-start = (f32[48,1,64,256]{3,2,1,0:T(8,128)S(1)}, f32[48,1,64,256]{3,2,1,0:T(8,128)}, u32[]{:S(2)}, u32[]{:S(2)}) collective-permute-start(f32[48,1,64,256]{3,2,1,0:T(8,128)S(1)} %get-tuple-element.10), channel_id=1, source_target_pairs={{0,2},{2,4},{4,6},{6,8},{8,10},{10,12},{12,14},{14,16},{16,18},{18... | collective-permute-start | bytes 9437192 | tf_op jit(solution)/shard_map/ppermute | solution.py:16
  19.4 136.8 %collective-permute-start.1 = (f32[48,1,64,256]{3,2,1,0:T(8,128)S(1)}, f32[48,1,64,256]{3,2,1,0:T(8,128)}, u32[]{:S(2)}, u32[]{:S(2)}) collective-permute-start(f32[48,1,64,256]{3,2,1,0:T(8,128)S(1)} %get-tuple-element.11), channel_id=1, source_target_pairs={{2,0},{4,2},{6,4},{8,6},{10,8},{12,10},{14,12},{16,14},{18,16},{20... | collective-permute-start | bytes 9437192 | tf_op jit(solution)/shard_map/ppermute | solution.py:19
  307.9 22.7 %copy-start.1 = (f32[16,48]{1,0:T(8,128)}, f32[16,48]{1,0:T(8,128)S(1)}, u32[]{:S(2)}) copy-start(f32[16,48]{1,0:T(8,128)S(1)} %fusion.31) | copy-start | bytes 9220
